TPU v7x, 32 devices: a whole 2x2x4 slice. The times are simulated.
32 devices in a mesh: smp: 8 (over z, y), var: 4 (over x, core).
Axes of the slice: x: 2, y: 2, z: 4, core: 2. Of those that a mesh axis runs over, the one named last changes fastest.
Arguments:
- dosage: int32 [512, 2048], P('smp', 'var'), may hold values from -2147483648 to 2147483647, as said below
- shares_init: float32 [12, 8192], P(None, ('smp', 'var')), may hold values from 0.1 to 1
- freqs_init: float32 [12, 2048], P(None, ('var', 'smp')), may hold values from 0.019 to 0.981
Outputs:
- shares: float32 [12, 8192], P(None, ('smp', 'var'))
- freqs: float32 [12, 2048], P(None, ('var', 'smp'))
Inputs may be any that keep to these rules, and one draw needn't show every extreme that they name: Every 2-bit code in a word of dosage is 0, 1, 2 or 3, and 3 marks a missing genotype.
All inputs are finite; a program needn't handle non-finite values.
Results may differ from a plain program's by a relative error of at most 0.0003.
Values sent between devices are 32-bit elements; how exact they have to be, the bound alone decides.
A program may use at most 64 MiB of HBM per device.

v0:
```python
import jax
import jax.numpy as jnp
from jax import lax
from jax.sharding import PartitionSpec as P

ITERS = 2
HIGH = lax.Precision.HIGHEST


def unpack_codes(packed):
    shifts = 2 * jnp.arange(16, dtype=jnp.int32)
    codes = jnp.bitwise_and(jnp.right_shift(packed[:, None, :], shifts[None, :, None]), 3)
    return codes.reshape(packed.shape[0] * 16, packed.shape[1])


def expect_sums(packed, shares_block, freqs_block):
    codes = unpack_codes(packed)
    live = (codes < 3).astype(jnp.float32)
    allele_f = live * codes.astype(jnp.float32)
    probs = jnp.einsum("kn,km->nm", shares_block, freqs_block, precision=HIGH)
    ratio_alt = allele_f / probs
    ratio_ref = (2.0 * live - allele_f) / (1.0 - probs)
    sum_q = jnp.einsum("km,nm->kn", freqs_block, ratio_alt, precision=HIGH) + jnp.einsum(
        "km,nm->kn", 1.0 - freqs_block, ratio_ref, precision=HIGH
    )
    sum_a = jnp.einsum("kn,nm->km", shares_block, ratio_alt, precision=HIGH)
    sum_b = jnp.einsum("kn,nm->km", shares_block, ratio_ref, precision=HIGH)
    return (sum_q, sum_a, sum_b)


def block_sums(packed, shares_block, freqs_block):
    word_rows = min(packed.shape[0], 16)
    blocks = packed.shape[0] // word_rows
    populations = shares_block.shape[0]
    packed_blocks = packed.reshape(blocks, word_rows, packed.shape[1])
    share_blocks = shares_block.reshape(populations, blocks, word_rows * 16).transpose(1, 0, 2)

    def one_block(carry, items):
        sum_q, sum_a, sum_b = expect_sums(items[0], items[1], freqs_block)
        return ((carry[0] + sum_a, carry[1] + sum_b), sum_q)

    start = (jnp.zeros(freqs_block.shape, jnp.float32), jnp.zeros(freqs_block.shape, jnp.float32))
    totals, sums_q = lax.scan(one_block, start, (packed_blocks, share_blocks))
    sum_q = sums_q.transpose(1, 0, 2).reshape(populations, shares_block.shape[1])
    return (sum_q, totals[0], totals[1])


def renew_shares(shares_block, sum_q):
    numer = shares_block * sum_q
    return (numer + 0.5) / (jnp.sum(numer, axis=0, keepdims=True) + 0.5 * shares_block.shape[0])


def renew_freqs(freqs_block, sum_a, sum_b):
    alt_part = freqs_block * sum_a
    ref_part = (1.0 - freqs_block) * sum_b
    return (alt_part + 0.5) / (alt_part + ref_part + 1.0)


def body(dosage, shares_init, freqs_init):
    own_shares = shares_init / jnp.sum(shares_init, axis=0, keepdims=True)
    own_freqs = freqs_init
    share_width = shares_init.shape[1]
    freq_width = freqs_init.shape[1]
    shares_block = lax.all_gather(own_shares, "var", axis=1, tiled=True)
    freqs_block = lax.all_gather(own_freqs, "smp", axis=1, tiled=True)
    for iteration in range(ITERS):
        part_q, part_a, part_b = block_sums(dosage, shares_block, freqs_block)
        sum_q = lax.psum(part_q, "var")
        sum_a, sum_b = lax.psum((part_a, part_b), "smp")
        shares_block = renew_shares(shares_block, sum_q)
        freqs_block = renew_freqs(freqs_block, sum_a, sum_b)
        if iteration + 1 == ITERS:
            own_shares = lax.dynamic_slice_in_dim(
                shares_block, lax.axis_index("var") * share_width, share_width, 1
            )
            own_freqs = lax.dynamic_slice_in_dim(
                freqs_block, lax.axis_index("smp") * freq_width, freq_width, 1
            )
    return (own_shares, own_freqs)


def solution(mesh):
    placed = (P("smp", "var"), P(None, ("smp", "var")), P(None, ("var", "smp")))
    return jax.shard_map(
        body,
        mesh=mesh,
        in_specs=placed,
        out_specs=(P(None, ("smp", "var")), P(None, ("var", "smp"))),
        check_vma=False,
    )
```

profile of v0, /device:TPU:0, one launch (start us, length us, event | category | flops | bytes accessed | tf_op | source)
XLA Modules:
  0.0 156.3 jit_solution(4070201371241163746)
XLA Ops:
  0.6 0.8 reduce_sum.27
  1.4 6.2 %all_gather.6 = f32[12,1024]{1,0:T(8,128)S(1)} all-gather(f32[12,256]{1,0:T(8,128)S(1)} %broadcast_divide_fusion), channel_id=1, replica_groups=mesh['smp'=8,'var'=4] {'var'}, dimensions={1}, use_global_device_ids=true | all-gather | bytes 61440 | tf_op jit(solution)/shard_map/all_gather | solution.py:64
  7.7 0.0 copy-start.2
  7.7 0.7 copy-done.2
  8.4 31.4 %all-gather = f32[8,64,12]{1,2,0:T(8,128)S(1)} all-gather(f32[1,64,12]{1,2,0:T(8,128)S(1)} %bitcast.171), channel_id=1, replica_groups=mesh['smp'=8,'var'=4] {'smp'}, dimensions={0}, use_global_device_ids=true | all-gather | bytes 27648 | tf_op jit(solution)/shard_map/all_gather | solution.py:65
  39.8 0.1 reshape.53
  39.9 0.8 copy-done
  40.7 10.8 %while.30 = (s32[]{:T(128)}, f32[12,512]{1,0:T(8,128)S(1)}, f32[12,512]{1,0:T(8,128)S(1)}, f32[4,12,256]{2,1,0:T(8,128)S(1)}, f32[4,12,256]{2,1,0:T(8,128)S(1)},...) while((s32[]{:T(128)}, f32[12,512]{1,0:T(8,128)S(1)}, ...), condition=%wide.region_2.3_spmd.clone, body=%wide.region_1.2_spmd.clone.sunk | while | flops 95716368 | bytes 3547396 | solution.py:43
  40.7 0.1 shift_right_arithmetic.118
  40.8 0.8 fusion.92
  41.6 0.4 convolution_add_fusion.10
  41.9 0.4 convolution_add_fusion.11
  42.3 0.5 convolution_bitcast_fusion.4
  42.8 0.5 fusion.93
  43.4 0.1 shift_right_arithmetic.118
  43.5 0.8 fusion.92
  44.2 0.4 convolution_add_fusion.10
  44.6 0.4 convolution_add_fusion.11
  45.0 0.5 convolution_bitcast_fusion.4
  45.5 0.5 fusion.93
  46.1 0.1 shift_right_arithmetic.118
  46.2 0.8 fusion.92
  46.9 0.4 convolution_add_fusion.10
  47.3 0.4 convolution_add_fusion.11
  47.7 0.5 convolution_bitcast_fusion.4
  48.2 0.5 fusion.93
  48.8 0.1 shift_right_arithmetic.118
  48.8 0.8 fusion.92
  49.6 0.4 convolution_add_fusion.10
  50.0 0.4 convolution_add_fusion.11
  50.4 0.5 convolution_bitcast_fusion.4
  50.9 0.5 fusion.93
  51.5 10.7 %psum.42 = f32[12,1024]{1,0:T(8,128)S(1)} all-reduce(f32[12,1024]{1,0:T(8,128)S(1)} %bitcast.169), channel_id=1, replica_groups=mesh['smp'=8,'var'=4] {'var'}, use_global_device_ids=true, to_apply=%region_3.4 | all-reduce | flops 12288 | bytes 98304 | tf_op jit(solution)/shard_map/psum | solution.py:68
  62.3 37.5 %all-reduce.1 = (f32[12,512]{1,0:T(8,128)S(1)}, f32[12,512]{1,0:T(8,128)S(1)}) all-reduce(f32[12,512]{1,0:T(8,128)S(1)} %get-tuple-element.82, f32[12,512]{1,0:T(8,128)S(1)} %get-tuple-element.81), channel_id=1, replica_groups=mesh['smp'=8,'var'=4] {'smp'}, use_global_device_ids=true, to_apply=%region_6.7 | all-reduce | flops 12288 | bytes 98304 | tf_op jit(solution)/shard_map/psum | solution.py:69
  99.9 10.8 %while.31 = (s32[]{:T(128)}, f32[12,512]{1,0:T(8,128)S(1)}, f32[12,512]{1,0:T(8,128)S(1)}, f32[4,12,256]{2,1,0:T(8,128)S(1)}, f32[4,12,256]{2,1,0:T(8,128)S(1)},...) while((s32[]{:T(128)}, f32[12,512]{1,0:T(8,128)S(1)}, ...), condition=%wide.region_8.9_spmd.clone, body=%wide.region_7.8_spmd.clone.sunk | while | flops 95716368 | bytes 3547396 | solution.py:43
  99.9 0.1 shift_right_arithmetic.123
  100.0 0.8 fusion.103
  100.8 0.4 convolution_add_fusion.12
  101.2 0.4 convolution_add_fusion.13
  101.5 0.5 convolution_bitcast_fusion.5
  102.1 0.5 fusion.104
  102.6 0.1 shift_right_arithmetic.123
  102.7 0.8 fusion.103
  103.5 0.4 convolution_add_fusion.12
  103.9 0.4 convolution_add_fusion.13
  104.2 0.5 convolution_bitcast_fusion.5
  104.8 0.5 fusion.104
  105.3 0.1 shift_right_arithmetic.123
  105.4 0.8 fusion.103
  106.2 0.4 convolution_add_fusion.12
  106.6 0.4 convolution_add_fusion.13
  106.9 0.5 convolution_bitcast_fusion.5
  107.5 0.5 fusion.104
  108.0 0.1 shift_right_arithmetic.123
  108.1 0.8 fusion.103
  108.9 0.4 convolution_add_fusion.12
  109.3 0.4 convolution_add_fusion.13
  109.6 0.5 convolution_bitcast_fusion.5
  110.2 0.5 fusion.104
  110.8 10.7 %psum.45 = f32[12,1024]{1,0:T(8,128)S(1)} all-reduce(f32[12,1024]{1,0:T(8,128)S(1)} %bitcast.170), channel_id=1, replica_groups=mesh['smp'=8,'var'=4] {'var'}, use_global_device_ids=true, to_apply=%region_9.10 | all-reduce | flops 12288 | bytes 98304 | tf_op jit(solution)/shard_map/psum | solution.py:68
  121.5 0.1 dynamic-slice
  121.6 0.6 fusion.44
  122.2 33.4 %all-reduce = (f32[12,512]{1,0:T(8,128)S(1)}, f32[12,512]{1,0:T(8,128)S(1)}) all-reduce(f32[12,512]{1,0:T(8,128)S(1)} %get-tuple-element.85, f32[12,512]{1,0:T(8,128)S(1)} %get-tuple-element.84), channel_id=1, replica_groups=mesh['smp'=8,'var'=4] {'smp'}, use_global_device_ids=true, to_apply=%region_12.13 | all-reduce | flops 12288 | bytes 98304 | tf_op jit(solution)/shard_map/psum | solution.py:69
  155.6 0.7 fusion.47
  (51 shorter events, 0.5 us)
Async XLA Ops:
  0.6 0.8 copy-start.1
  7.7 0.7 copy-start.2
  39.8 0.9 copy-start
where the time goes:
time: 157 us; the launch traced here: 156 us
  blocking collectives  130 us (83%)
  matrix products  20.5 us (13%)
  local copies, waits for them, and re-layouts  2.55 us (2%)
  other arithmetic  2.3 us (1%)
    psum x2, blocking collectives, body(): sum_a, sum_b = lax.psum((part_a, part_b), 'smp')  70.9 us
    all_gather x1, blocking collectives, body(): freqs_block = lax.all_gather(own_freqs, 'smp', axis=1, tiled=True)  31.4 us
    psum x2, blocking collectives, body(): sum_q = lax.psum(part_q, 'var')  21.3 us
    dot_general x8, matrix products, expect_sums(): probs = jnp.einsum('kn,km->nm', shares_block, freqs_block, precision=HIGH)  6.22 us
    all_gather x1, blocking collectives, body(): shares_block = lax.all_gather(own_shares, 'var', axis=1, tiled=True)  6.22 us
    dot_general x8, matrix products, expect_sums(): jnp.einsum('km,nm->kn', 1.0 - freqs_block, ratio_ref, precision=HIGH)  4.22 us
    dot_general x8, matrix products, expect_sums(): jnp.einsum('km,nm->kn', freqs_block, ratio_alt, precision=HIGH)  4.14 us

commit v1 on v0

--- a/solution.py
+++ b/solution.py
@@ -5,6 +5,14 @@
 
 ITERS = 2
 HIGH = lax.Precision.HIGHEST
+
+
+def added_up(block, axis):
+    n_dev, summed = (lax.axis_size(axis), block)
+    for far in [1 << k for k in range(n_dev.bit_length() - 1)]:
+        swap = [(i, i ^ far) for i in range(n_dev)]
+        summed = summed + lax.ppermute(summed, axis, swap)
+    return summed
 
 
 def unpack_codes(packed):
@@ -65,7 +73,7 @@
     freqs_block = lax.all_gather(own_freqs, "smp", axis=1, tiled=True)
     for iteration in range(ITERS):
         part_q, part_a, part_b = block_sums(dosage, shares_block, freqs_block)
-        sum_q = lax.psum(part_q, "var")
+        sum_q = added_up(part_q, "var")
         sum_a, sum_b = lax.psum((part_a, part_b), "smp")
         shares_block = renew_shares(shares_block, sum_q)
         freqs_block = renew_freqs(freqs_block, sum_a, sum_b)

time: 157 us -> 143 us (0.911)
  blocking collectives: 130 us -> 108 us
  waiting for transfers between devices: 0 us -> 4.84 us
  starting transfers between devices: 0 us -> 3.25 us
    psum x2 -> x0, blocking collectives: 21.3 us -> none  [body(): sum_q = lax.psum(part_q, 'var')]
    ppermute x0 -> x4, waiting for transfers between devices: none -> 4.84 us  [added_up(): summed = summed + lax.ppermute(summed, axis, swap)]
    ppermute x0 -> x4, starting transfers between devices: none -> 3.25 us  [added_up(): summed = summed + lax.ppermute(summed, axis, swap)]
  transfers between devices with their start and end apart: 0 -> 4, of which waited for: 0 -> 2; matrix products, arithmetic and copies ran while one was open for 0% -> 0% of each run, Pallas kernels for 0% -> 0%
where the time goes in v1:
time: 143 us
  blocking collectives  108 us (76%)
  matrix products  20.5 us (14%)
  waiting for transfers between devices  4.84 us (3%)
  starting transfers between devices  3.25 us (2%)
  local copies, waits for them, and re-layouts  2.55 us (2%)
  other arithmetic  2.3 us (2%)
    psum x2, blocking collectives, body(): sum_a, sum_b = lax.psum((part_a, part_b), 'smp')  70.9 us
    all_gather x1, blocking collectives, body(): freqs_block = lax.all_gather(own_freqs, 'smp', axis=1, tiled=True)  31.4 us
    dot_general x8, matrix products, expect_sums(): probs = jnp.einsum('kn,km->nm', shares_block, freqs_block, precision=HIGH)  6.22 us
    all_gather x1, blocking collectives, body(): shares_block = lax.all_gather(own_shares, 'var', axis=1, tiled=True)  6.22 us
    ppermute x4, waiting for transfers between devices, added_up(): summed = summed + lax.ppermute(summed, axis, swap)  4.84 us
    dot_general x8, matrix products, expect_sums(): jnp.einsum('km,nm->kn', 1.0 - freqs_block, ratio_ref, precision=HIGH)  4.22 us
    dot_general x8, matrix products, expect_sums(): jnp.einsum('km,nm->kn', freqs_block, ratio_alt, precision=HIGH)  4.14 us
    ppermute x4, starting transfers between devices, added_up(): summed = summed + lax.ppermute(summed, axis, swap)  3.25 us
  transfers between devices with their start and end apart: 4, of which 2 were waited for; matrix products, arithmetic and copies ran while one was open for 0% of the time, Pallas kernels for 0%

profile of v1, /device:TPU:0, one launch (start us, length us, event | category | flops | bytes accessed | tf_op | source)
XLA Modules:
  0.0 143.1 jit_solution(13478180852487959215)
XLA Ops:
  0.7 0.8 reduce_sum.27
  1.5 6.2 %all_gather.6 = f32[12,1024]{1,0:T(8,128)S(1)} all-gather(f32[12,256]{1,0:T(8,128)S(1)} %broadcast_divide_fusion), channel_id=1, replica_groups=mesh['smp'=8,'var'=4] {'var'}, dimensions={1}, use_global_device_ids=true | all-gather | bytes 61440 | tf_op jit(solution)/shard_map/all_gather | solution.py:72
  7.7 0.7 copy-done.2
  8.4 31.4 %all-gather = f32[8,64,12]{1,2,0:T(8,128)S(1)} all-gather(f32[1,64,12]{1,2,0:T(8,128)S(1)} %bitcast.173), channel_id=1, replica_groups=mesh['smp'=8,'var'=4] {'smp'}, dimensions={0}, use_global_device_ids=true | all-gather | bytes 27648 | tf_op jit(solution)/shard_map/all_gather | solution.py:73
  39.9 0.8 copy-done
  40.7 10.8 %while.30 = (s32[]{:T(128)}, f32[12,512]{1,0:T(8,128)S(1)}, f32[12,512]{1,0:T(8,128)S(1)}, f32[4,12,256]{2,1,0:T(8,128)S(1)}, f32[4,12,256]{2,1,0:T(8,128)S(1)},...) while((s32[]{:T(128)}, f32[12,512]{1,0:T(8,128)S(1)}, ...), condition=%wide.region_2.3_spmd.clone, body=%wide.region_1.2_spmd.clone.sunk | while | flops 95716368 | bytes 3547396 | solution.py:51
  40.7 0.1 shift_right_arithmetic.118
  40.8 0.8 fusion.93
  41.6 0.4 convolution_add_fusion.10
  41.9 0.4 convolution_add_fusion.11
  42.3 0.5 convolution_bitcast_fusion.4
  42.8 0.5 fusion.94
  43.4 0.1 shift_right_arithmetic.118
  43.5 0.8 fusion.93
  44.2 0.4 convolution_add_fusion.10
  44.6 0.4 convolution_add_fusion.11
  45.0 0.5 convolution_bitcast_fusion.4
  45.5 0.5 fusion.94
  46.1 0.1 shift_right_arithmetic.118
  46.2 0.8 fusion.93
  46.9 0.4 convolution_add_fusion.10
  47.3 0.4 convolution_add_fusion.11
  47.7 0.5 convolution_bitcast_fusion.4
  48.2 0.5 fusion.94
  48.8 0.1 shift_right_arithmetic.118
  48.8 0.8 fusion.93
  49.6 0.4 convolution_add_fusion.10
  50.0 0.4 convolution_add_fusion.11
  50.4 0.5 convolution_bitcast_fusion.4
  50.9 0.5 fusion.94
  51.6 37.5 %all-reduce.1 = (f32[12,512]{1,0:T(8,128)S(1)}, f32[12,512]{1,0:T(8,128)S(1)}) all-reduce(f32[12,512]{1,0:T(8,128)S(1)} %get-tuple-element.82, f32[12,512]{1,0:T(8,128)S(1)} %get-tuple-element.81), channel_id=1, replica_groups=mesh['smp'=8,'var'=4] {'smp'}, use_global_device_ids=true, to_apply=%region_5.6 | all-reduce | flops 12288 | bytes 98304 | tf_op jit(solution)/shard_map/psum | solution.py:77
  89.2 1.6 %collective-permute-start.1 = (f32[12,1024]{1,0:T(8,128)S(1)}, f32[12,1024]{1,0:T(8,128)S(1)}, u32[]{:S(2)}, u32[]{:S(2)}) collective-permute-start(f32[12,1024]{1,0:T(8,128)S(1)} %add.90), channel_id=1, source_target_pairs={{0,2},{1,3},{2,0},{3,1},{4,6},{5,7},{6,4},{7,5},{8,10},{9,11},{10,... | collective-permute-start | bytes 147464 | tf_op jit(solution)/shard_map/ppermute | solution.py:14
  90.8 2.7 %collective-permute-done.1 = f32[12,1024]{1,0:T(8,128)S(1)} collective-permute-done((f32[12,1024]{1,0:T(8,128)S(1)}, f32[12,1024]{1,0:T(8,128)S(1)}, u32[]{:S(2)}, u32[]{:S(2)}) %collective-permute-start.1) | collective-permute-done | bytes 49184 | tf_op jit(solution)/shard_map/ppermute | solution.py:14
  93.6 10.8 %while.31 = (s32[]{:T(128)}, f32[12,512]{1,0:T(8,128)S(1)}, f32[12,512]{1,0:T(8,128)S(1)}, f32[4,12,256]{2,1,0:T(8,128)S(1)}, f32[4,12,256]{2,1,0:T(8,128)S(1)},...) while((s32[]{:T(128)}, f32[12,512]{1,0:T(8,128)S(1)}, ...), condition=%wide.region_7.8_spmd.clone, body=%wide.region_6.7_spmd.clone.sunk | while | flops 95716368 | bytes 3547396 | solution.py:51
  93.7 0.1 shift_right_arithmetic.123
  93.7 0.8 fusion.104
  94.5 0.4 convolution_add_fusion.12
  94.9 0.4 convolution_add_fusion.13
  95.3 0.5 convolution_bitcast_fusion.5
  95.8 0.5 fusion.105
  96.3 0.1 shift_right_arithmetic.123
  96.4 0.8 fusion.104
  97.2 0.4 convolution_add_fusion.12
  97.6 0.4 convolution_add_fusion.13
  98.0 0.5 convolution_bitcast_fusion.5
  98.5 0.5 fusion.105
  99.0 0.1 shift_right_arithmetic.123
  99.1 0.8 fusion.104
  99.9 0.4 convolution_add_fusion.12
  100.3 0.4 convolution_add_fusion.13
  100.7 0.5 convolution_bitcast_fusion.5
  101.2 0.5 fusion.105
  101.7 0.1 shift_right_arithmetic.123
  101.8 0.8 fusion.104
  102.6 0.4 convolution_add_fusion.12
  103.0 0.4 convolution_add_fusion.13
  103.4 0.5 convolution_bitcast_fusion.5
  103.9 0.5 fusion.105
  104.6 33.4 %all-reduce = (f32[12,512]{1,0:T(8,128)S(1)}, f32[12,512]{1,0:T(8,128)S(1)}) all-reduce(f32[12,512]{1,0:T(8,128)S(1)} %get-tuple-element.85, f32[12,512]{1,0:T(8,128)S(1)} %get-tuple-element.84), channel_id=1, replica_groups=mesh['smp'=8,'var'=4] {'smp'}, use_global_device_ids=true, to_apply=%region_10.11 | all-reduce | flops 12288 | bytes 98304 | tf_op jit(solution)/shard_map/psum | solution.py:77
  138.0 1.6 %collective-permute-start.3 = (f32[12,1024]{1,0:T(8,128)S(1)}, f32[12,1024]{1,0:T(8,128)S(1)}, u32[]{:S(2)}, u32[]{:S(2)}) collective-permute-start(f32[12,1024]{1,0:T(8,128)S(1)} %add.97), channel_id=1, source_target_pairs={{0,2},{1,3},{2,0},{3,1},{4,6},{5,7},{6,4},{7,5},{8,10},{9,11},{10,... | collective-permute-start | bytes 147464 | tf_op jit(solution)/shard_map/ppermute | solution.py:14
  139.6 0.7 fusion.47
  140.3 2.1 %collective-permute-done.3 = f32[12,1024]{1,0:T(8,128)S(1)} collective-permute-done((f32[12,1024]{1,0:T(8,128)S(1)}, f32[12,1024]{1,0:T(8,128)S(1)}, u32[]{:S(2)}, u32[]{:S(2)}) %collective-permute-start.3) | collective-permute-done | bytes 49184 | tf_op jit(solution)/shard_map/ppermute | solution.py:14
  142.4 0.1 dynamic-slice
  142.5 0.6 fusion.44
  (59 shorter events, 0.7 us)
Async XLA Ops:
  0.6 0.8 copy-start.1
  7.7 0.7 copy-start.2
  39.8 0.9 copy-start
  51.5 37.6 %collective-permute-start = (f32[12,1024]{1,0:T(8,128)S(1)}, f32[12,1024]{1,0:T(8,128)S(1)}, u32[]{:S(2)}, u32[]{:S(2)}) collective-permute-start(f32[12,1024]{1,0:T(8,128)S(1)} %bitcast.167), channel_id=1, source_target_pairs={{0,1},{1,0},{2,3},{3,2},{4,5},{5,4},{6,7},{7,6},{8,9},{9,8},{10,11... | collective-permute-start | bytes 147464 | tf_op jit(solution)/shard_map/ppermute | solution.py:14
  89.2 4.3 %collective-permute-start.1 = (f32[12,1024]{1,0:T(8,128)S(1)}, f32[12,1024]{1,0:T(8,128)S(1)}, u32[]{:S(2)}, u32[]{:S(2)}) collective-permute-start(f32[12,1024]{1,0:T(8,128)S(1)} %add.90), channel_id=1, source_target_pairs={{0,2},{1,3},{2,0},{3,1},{4,6},{5,7},{6,4},{7,5},{8,10},{9,11},{10,... | collective-permute-start | bytes 147464 | tf_op jit(solution)/shard_map/ppermute | solution.py:14
  104.5 33.5 %collective-permute-start.2 = (f32[12,1024]{1,0:T(8,128)S(1)}, f32[12,1024]{1,0:T(8,128)S(1)}, u32[]{:S(2)}, u32[]{:S(2)}) collective-permute-start(f32[12,1024]{1,0:T(8,128)S(1)} %bitcast.165), channel_id=1, source_target_pairs={{0,1},{1,0},{2,3},{3,2},{4,5},{5,4},{6,7},{7,6},{8,9},{9,8},{10,11... | collective-permute-start | bytes 147464 | tf_op jit(solution)/shard_map/ppermute | solution.py:14
  138.0 4.3 %collective-permute-start.3 = (f32[12,1024]{1,0:T(8,128)S(1)}, f32[12,1024]{1,0:T(8,128)S(1)}, u32[]{:S(2)}, u32[]{:S(2)}) collective-permute-start(f32[12,1024]{1,0:T(8,128)S(1)} %add.97), channel_id=1, source_target_pairs={{0,2},{1,3},{2,0},{3,1},{4,6},{5,7},{6,4},{7,5},{8,10},{9,11},{10,... | collective-permute-start | bytes 147464 | tf_op jit(solution)/shard_map/ppermute | solution.py:14
